TPU v7x, 32 devices: a whole 2x2x4 slice. The times are simulated.
32 devices in a mesh: ctx: 4 (over z), fsdp: 8 (over y, x, core).
Axes of the slice: x: 2, y: 2, z: 4, core: 2. Of those that a mesh axis runs over, the one named last changes fastest.
Arguments:
- tokens_in: bfloat16 [8, 4096, 768], P('fsdp', 'ctx'), may hold values from -6 to 6
- out_grad: bfloat16 [8, 4096, 768], P('fsdp', 'ctx'), may hold values from -6 to 6
- gain_attn: bfloat16 [768], P('fsdp'), may hold values from 0.5 to 1.5
- gain_mlp: bfloat16 [768], P('fsdp'), may hold values from 0.5 to 1.5
- w_qkv: bfloat16 [768, 2304], P('fsdp'), may hold values from -0.21875 to 0.21875
- w_out: bfloat16 [768, 768], P('fsdp'), may hold values from -6 to 6
- w_up: bfloat16 [768, 3072], P('fsdp'), may hold values from -0.21875 to 0.21875
- w_down: bfloat16 [3072, 768], P('fsdp'), may hold values from -0.109375 to 0.109375
- lengths: int32 [8], P('fsdp'), may hold values from 1024 to 4096, as said below
- block_order: int32 [8, 8], P('fsdp'), may hold values from 0 to 7, as said below
Outputs:
- result: bfloat16 [8, 4096, 768], P('fsdp', 'ctx')
- grad_tokens: bfloat16 [8, 4096, 768], P('fsdp', 'ctx')
- grad_gain_attn: float32 [768], P('fsdp')
- grad_gain_mlp: float32 [768], P('fsdp')
- grad_w_qkv: float32 [768, 2304], P('fsdp')
- grad_w_out: float32 [768, 768], P('fsdp')
- grad_w_up: float32 [768, 3072], P('fsdp')
- grad_w_down: float32 [3072, 768], P('fsdp')
Inputs may be any that keep to these rules, and one draw needn't show every extreme that they name: `lengths`: some sequence has exactly 4096 valid tokens and some exactly 1024. `block_order`: each row holds every block number once; stored blocks 2 c and 2 c + 1 of a row are block numbers p and 7 - p in some order, for some p.
All inputs are finite; a program needn't handle non-finite values.
Results may differ from a plain program's by a relative error of at most 0.015.
The roundings to bfloat16 on the way count: a program that leaves them out, or rounds other values in their place, can miss the bound.
Values may be sent and summed in bfloat16 or wider, within the bound.
A program may use at most 256 MiB of HBM per device.

v0:
```python
import jax
import jax.numpy as jnp
from jax import lax
from jax.sharding import PartitionSpec as P

HEAD_DIM = 64
BLK = 512


def layer_norm(values, gain):
    centre = jnp.mean(values, axis=-1, keepdims=True)
    centred = values - centre
    spread = jnp.mean(centred * centred, axis=-1, keepdims=True)
    return centred * lax.rsqrt(spread + 1e-05) * gain


def gelu_tanh(values):
    return jax.nn.gelu(values, approximate=True)


def project(left_operand, right_operand):
    return jnp.einsum(
        "buj,jn->bun", left_operand, right_operand, preferred_element_type=jnp.float32
    )


def project_back(gradient_list, right_operand):
    return jnp.einsum(
        "mzg,og->mzo", gradient_list, right_operand, preferred_element_type=jnp.float32
    )


def weight_grad(left_operand, gradient_list):
    return jnp.einsum(
        "hcb,hct->bt", left_operand, gradient_list, preferred_element_type=jnp.float32
    )


def attend_forward(query_seq, key_all, value_all, query_places, key_places, length):
    local_rows, width = query_seq.shape
    slot_count = key_all.shape[0]
    pair_width = 2 * HEAD_DIM
    pair_total = width // pair_width
    block_total = local_rows // BLK
    score_scale = HEAD_DIM ** (-0.5)
    key_live = key_places < length

    def one_pair(pair_id, buffers):
        out_rows, log_totals = buffers
        column = pair_id * pair_width
        keys_pair = lax.dynamic_slice_in_dim(key_all, column, pair_width, 1).reshape(
            slot_count, 2, HEAD_DIM
        )
        values_pair = lax.dynamic_slice_in_dim(value_all, column, pair_width, 1).reshape(
            slot_count, 2, HEAD_DIM
        )
        for block_id in range(block_total):
            query_rows = lax.dynamic_slice(
                query_seq, (block_id * BLK, column), (BLK, pair_width)
            ).reshape(BLK, 2, HEAD_DIM)
            row_places = query_places[block_id * BLK : (block_id + 1) * BLK]
            allowed = (key_places[None, :] <= row_places[:, None]) & key_live[None, :]
            scores = (
                jnp.einsum(
                    "qhe,khe->hqk", query_rows, keys_pair, preferred_element_type=jnp.float32
                )
                * score_scale
            )
            magnitude = jnp.abs(scores)
            row_top = jnp.max(jnp.where(allowed, magnitude, -1e30), axis=-1, keepdims=True)
            exponent = jnp.where(allowed, jnp.exp(magnitude - row_top), 0.0)
            row_total = jnp.sum(exponent, axis=-1, keepdims=True)
            signed = (jnp.sign(scores) * (exponent / row_total)).astype(jnp.bfloat16)
            mixture = jnp.einsum(
                "hqk,khe->qhe", signed, values_pair, preferred_element_type=jnp.float32
            )
            mixture = mixture.reshape(BLK, pair_width).astype(jnp.bfloat16)
            out_rows = lax.dynamic_update_slice(out_rows, mixture, (block_id * BLK, column))
            block_logs = (row_top + jnp.log(row_total))[None, None, :, :, 0]
            log_totals = lax.dynamic_update_slice(log_totals, block_logs, (block_id, pair_id, 0, 0))
        return (out_rows, log_totals)

    start = (
        jnp.zeros((local_rows, width), jnp.bfloat16),
        jnp.zeros((block_total, pair_total, 2, BLK), jnp.float32),
    )
    return lax.fori_loop(0, pair_total, one_pair, start)


def attend_backward(
    query_seq, key_all, value_all, grad_out, log_totals, query_places, key_places, length
):
    local_rows, width = query_seq.shape
    slot_count = key_all.shape[0]
    pair_width = 2 * HEAD_DIM
    pair_total = width // pair_width
    block_total = local_rows // BLK
    score_scale = HEAD_DIM ** (-0.5)
    key_live = key_places < length

    def one_pair(pair_id, buffers):
        query_grads, row_dots = (buffers[0], buffers[1])
        column = pair_id * pair_width
        keys_pair = lax.dynamic_slice_in_dim(key_all, column, pair_width, 1).reshape(
            slot_count, 2, HEAD_DIM
        )
        values_pair = lax.dynamic_slice_in_dim(value_all, column, pair_width, 1).reshape(
            slot_count, 2, HEAD_DIM
        )
        key_part = jnp.zeros((slot_count, 2, HEAD_DIM), jnp.float32)
        value_part = jnp.zeros((slot_count, 2, HEAD_DIM), jnp.float32)
        for block_id in range(block_total):
            query_rows = lax.dynamic_slice(
                query_seq, (block_id * BLK, column), (BLK, pair_width)
            ).reshape(BLK, 2, HEAD_DIM)
            grad_rows = lax.dynamic_slice(
                grad_out, (block_id * BLK, column), (BLK, pair_width)
            ).reshape(BLK, 2, HEAD_DIM)
            row_places = query_places[block_id * BLK : (block_id + 1) * BLK]
            allowed = (key_places[None, :] <= row_places[:, None]) & key_live[None, :]
            scores = (
                jnp.einsum(
                    "qhe,khe->hqk", query_rows, keys_pair, preferred_element_type=jnp.float32
                )
                * score_scale
            )
            block_logs = log_totals[block_id, pair_id]
            positive = jnp.where(allowed, jnp.exp(jnp.abs(scores) - block_logs[:, :, None]), 0.0)
            signed = jnp.sign(scores) * positive
            weight_grads = jnp.einsum(
                "qhe,khe->hqk", grad_rows, values_pair, preferred_element_type=jnp.float32
            )
            row_dot = jnp.sum(signed * weight_grads, axis=-1, keepdims=True)
            score_grads = (positive * weight_grads - signed * row_dot).astype(jnp.bfloat16)
            query_part = (
                jnp.einsum(
                    "hqk,khe->qhe", score_grads, keys_pair, preferred_element_type=jnp.float32
                )
                * score_scale
            )
            query_grads = lax.dynamic_update_slice(
                query_grads, query_part.reshape(BLK, pair_width), (block_id * BLK, column)
            )
            row_dots = lax.dynamic_update_slice(
                row_dots, row_dot[None, None, :, :, 0], (block_id, pair_id, 0, 0)
            )
            value_part = value_part + jnp.einsum(
                "hqk,qhe->khe",
                signed.astype(jnp.bfloat16),
                grad_rows,
                preferred_element_type=jnp.float32,
            )
            key_part = (
                key_part
                + jnp.einsum(
                    "hqk,qhe->khe", score_grads, query_rows, preferred_element_type=jnp.float32
                )
                * score_scale
            )
        key_gradients = lax.dynamic_update_slice(
            buffers[2], key_part.reshape(slot_count, pair_width), (0, column)
        )
        value_grads = lax.dynamic_update_slice(
            buffers[3], value_part.reshape(slot_count, pair_width), (0, column)
        )
        return (query_grads, row_dots, key_gradients, value_grads)

    start = (
        jnp.zeros((local_rows, width), jnp.float32),
        jnp.zeros((block_total, pair_total, 2, BLK), jnp.float32),
    )
    start = start + (
        jnp.zeros((slot_count, width), jnp.float32),
        jnp.zeros((slot_count, width), jnp.float32),
    )
    return lax.fori_loop(0, pair_total, one_pair, start)


def per_device(
    tokens_in, out_grad, gain_attn, gain_mlp, w_qkv, w_out, w_up, w_down, lengths, block_order
):
    seq_count, local_rows, width = tokens_in.shape
    ctx_index = lax.axis_index("ctx")
    gain_one, w_qkv_all, w_out_all = (
        lax.all_gather(gain_attn, "fsdp", axis=0, tiled=True),
        lax.all_gather(w_qkv, "fsdp", axis=0, tiled=True),
        lax.all_gather(w_out, "fsdp", axis=0, tiled=True),
    )
    offsets = jnp.arange(BLK, dtype=jnp.int32)
    key_places = (block_order[:, :, None] * BLK + offsets[None, None, :]).reshape(seq_count, -1)
    query_places = lax.dynamic_slice_in_dim(key_places, ctx_index * local_rows, local_rows, 1)
    tokens_f = tokens_in.astype(jnp.float32)
    normed_one, norm_one_back = jax.vjp(layer_norm, tokens_f, gain_one.astype(jnp.float32))
    normed_one = normed_one.astype(jnp.bfloat16)
    packed = project(normed_one, w_qkv_all).astype(jnp.bfloat16)
    query_all = packed[:, :, :width]
    key_local = packed[:, :, width : 2 * width]
    value_local = packed[:, :, 2 * width :]
    key_all, value_all = (
        lax.all_gather(key_local, "ctx", axis=1, tiled=True),
        lax.all_gather(value_local, "ctx", axis=1, tiled=True),
    )
    seq_id = 0
    mixture, log_totals = attend_forward(
        query_all[seq_id],
        key_all[seq_id],
        value_all[seq_id],
        query_places[seq_id],
        key_places[seq_id],
        lengths[seq_id],
    )
    mixed_list = [mixture]
    logs_list = [log_totals]
    mixed = jnp.stack(mixed_list)
    middle = tokens_f + project(mixed, w_out_all)
    gain_two, w_up_all, w_down_all = (
        lax.all_gather(gain_mlp, "fsdp", axis=0, tiled=True),
        lax.all_gather(w_up, "fsdp", axis=0, tiled=True),
        lax.all_gather(w_down, "fsdp", axis=0, tiled=True),
    )
    normed_two, norm_two_back = jax.vjp(layer_norm, middle, gain_two.astype(jnp.float32))
    normed_two = normed_two.astype(jnp.bfloat16)
    pre_act = project(normed_two, w_up_all)
    activation, gelu_back = jax.vjp(gelu_tanh, pre_act)
    activation = activation.astype(jnp.bfloat16)
    result = (middle + project(activation, w_down_all)).astype(jnp.bfloat16)
    w_up_back, w_down_back = (
        lax.all_gather(w_up, "fsdp", axis=0, tiled=True),
        lax.all_gather(w_down, "fsdp", axis=0, tiled=True),
    )
    live_mask = (query_places < lengths[:, None]).astype(jnp.float32)
    output_gradient = out_grad.astype(jnp.float32) * live_mask[:, :, None]
    grad_z = output_gradient.astype(jnp.bfloat16)
    grad_w_down = weight_grad(activation, grad_z)
    grad_act = project_back(grad_z, w_down_back)
    grad_pre = gelu_back(grad_act)[0].astype(jnp.bfloat16)
    grad_w_up = weight_grad(normed_two, grad_pre)
    grad_normed_two = project_back(grad_pre, w_up_back)
    grad_middle_norm, grad_gain_two = norm_two_back(grad_normed_two)
    mlp_shards = (
        lax.psum_scatter(grad_w_up, "fsdp", scatter_dimension=0, tiled=True),
        lax.psum_scatter(grad_w_down, "fsdp", scatter_dimension=0, tiled=True),
        lax.psum_scatter(grad_gain_two, "fsdp", scatter_dimension=0, tiled=True),
    )
    grad_middle = output_gradient + grad_middle_norm
    w_qkv_back, w_out_back = (
        lax.all_gather(w_qkv, "fsdp", axis=0, tiled=True),
        lax.all_gather(w_out, "fsdp", axis=0, tiled=True),
    )
    grad_branch = grad_middle.astype(jnp.bfloat16)
    grad_w_out = weight_grad(mixed, grad_branch)
    grad_mixed = project_back(grad_branch, w_out_back).astype(jnp.bfloat16)
    seq_id = 0
    query_grads, row_dots, key_gradients, value_grads = attend_backward(
        query_all[seq_id],
        key_all[seq_id],
        value_all[seq_id],
        grad_mixed[seq_id],
        logs_list[seq_id],
        query_places[seq_id],
        key_places[seq_id],
        lengths[seq_id],
    )
    key_mine = lax.psum_scatter(
        key_gradients.astype(jnp.bfloat16), "ctx", scatter_dimension=0, tiled=True
    ).astype(jnp.float32)
    value_mine = lax.psum_scatter(
        value_grads.astype(jnp.bfloat16), "ctx", scatter_dimension=0, tiled=True
    ).astype(jnp.float32)
    packed_items = [jnp.concatenate([query_grads, key_mine, value_mine], axis=-1)]
    grad_packed = jnp.stack(packed_items).astype(jnp.bfloat16)
    grad_w_qkv = weight_grad(normed_one, grad_packed)
    grad_normed_one = project_back(grad_packed, w_qkv_back)
    grad_tokens_norm, grad_gain_one = norm_one_back(grad_normed_one)
    grad_tokens = (grad_middle + grad_tokens_norm).astype(jnp.bfloat16)
    attn_shards = (
        lax.psum_scatter(grad_w_qkv, "fsdp", scatter_dimension=0, tiled=True),
        lax.psum_scatter(grad_w_out, "fsdp", scatter_dimension=0, tiled=True),
        lax.psum_scatter(grad_gain_one, "fsdp", scatter_dimension=0, tiled=True),
    )
    summed = (
        lax.psum(attn_shards[0].astype(jnp.bfloat16), "ctx").astype(jnp.float32),
        lax.psum(attn_shards[1].astype(jnp.bfloat16), "ctx").astype(jnp.float32),
        lax.psum(attn_shards[2].astype(jnp.bfloat16), "ctx").astype(jnp.float32),
        lax.psum(mlp_shards[0].astype(jnp.bfloat16), "ctx").astype(jnp.float32),
        lax.psum(mlp_shards[1].astype(jnp.bfloat16), "ctx").astype(jnp.float32),
        lax.psum(mlp_shards[2].astype(jnp.bfloat16), "ctx").astype(jnp.float32),
    )
    return (result, grad_tokens, summed[2], summed[5], summed[0], summed[1], summed[3], summed[4])


def solution(mesh):
    return jax.shard_map(
        per_device,
        mesh=mesh,
        in_specs=(
            P("fsdp", "ctx", None),
            P("fsdp", "ctx", None),
            P("fsdp"),
            P("fsdp"),
            P("fsdp", None),
            P("fsdp", None),
            P("fsdp", None),
            P("fsdp", None),
            P("fsdp"),
            P("fsdp", None),
        ),
        out_specs=(
            P("fsdp", "ctx", None),
            P("fsdp", "ctx", None),
            P("fsdp"),
            P("fsdp"),
            P("fsdp", None),
            P("fsdp", None),
            P("fsdp", None),
            P("fsdp", None),
        ),
        check_vma=False,
    )
```

profile of v0, /device:TPU:0, one launch (start us, length us, event | category | flops | bytes accessed | tf_op | source)
XLA Modules:
  0.0 2123.5 jit_solution(18351826419260422261)
XLA Ops:
  30.3 16.2 all-gather.7.cloned.1.call-done
  62.7 107.6 %all-gather.11.cloned.1.call-done = bf16[1,4096,768]{2,1,0:T(8,128)(2,1)} async-done(((bf16[1,1024,768]{2,1,0:T(8,128)(2,1)}), bf16[1,4096,768]{2,1,0:T(8,128)(2,1)}) %all-gather.11.cloned.1.call-update) | async-done | bytes 6291472 | tf_op jit(solution)/shard_map/all_gather | solution.py:200
  179.2 106.9 %all-gather.9.cloned.1.call-done = bf16[1,4096,768]{2,1,0:T(8,128)(2,1)} async-done(((bf16[1,1024,768]{2,1,0:T(8,128)(2,1)}), bf16[1,4096,768]{2,1,0:T(8,128)(2,1)}) %all-gather.9.cloned.1.call-update) | async-done | bytes 6291472 | tf_op jit(solution)/shard_map/all_gather | solution.py:201
  296.2 364.7 %while.36 = (s32[]{:T(128)}, bf16[1024,768]{0,1:T(8,128)(2,1)}, f32[2,6,2,512]{3,2,1,0:T(2,128)}, bf16[4096,768]{0,1:T(8,128)(2,1)}, bf16[1024,768]{0,1:T(8,128)...) while((s32[]{:T(128)}, bf16[1024,768]{0,1:T(8,128)(2,1)}, ...), condition=%wide.region_7.8_spmd.clone.clone, body=%wide.region_2.7_spmd.clone.clone.sunk | while | flops 2298619904 | bytes 136040752 | solution.py:87
  717.7 814.1 %while.37 = (s32[]{:T(128)}, bf16[1024,768]{0,1:T(8,128)(2,1)}, bf16[4096,768]{0,1:T(8,128)(2,1)}, bf16[4096,768]{0,1:T(8,128)(2,1)}, bf16[4096,768]{0,1:T(8,128...) while((s32[]{:T(128)}, bf16[1024,768]{0,1:T(8,128)(2,1)}, ...), condition=%wide.region_15.16_spmd.clone.clone, body=%wide.region_12.15_spmd.clone.clone.sunk | while | flops 5589706752 | bytes 380612992 | solution.py:176
  747.8 18.6 multiply_reduce_fusion.6
  766.4 16.0 subtract_convert_fusion.5
  807.5 18.9 multiply_reduce_fusion.5
  826.4 16.2 subtract_convert_fusion.4
  882.1 18.6 multiply_reduce_fusion.6
  900.7 16.2 subtract_convert_fusion.5
  942.1 18.8 multiply_reduce_fusion.5
  1016.5 18.6 multiply_reduce_fusion.6
  1076.2 18.9 multiply_reduce_fusion.5
  1095.1 16.2 subtract_convert_fusion.4
  1150.8 18.6 multiply_reduce_fusion.6
  1169.4 16.2 subtract_convert_fusion.5
  1210.8 18.8 multiply_reduce_fusion.5
  1229.5 16.0 subtract_convert_fusion.4
  1285.2 18.6 multiply_reduce_fusion.6
  1345.0 18.9 multiply_reduce_fusion.5
  1363.8 16.2 subtract_convert_fusion.4
  1419.5 18.6 multiply_reduce_fusion.6
  1438.1 16.2 subtract_convert_fusion.5
  1479.5 18.8 multiply_reduce_fusion.5
  1563.2 77.2 %reduce-scatter.9.cloned.1.call-done = bf16[1024,768]{0,1:T(8,128)(2,1)} async-done(((bf16[4096,768]{0,1:T(8,128)(2,1)}), bf16[1024,768]{0,1:T(8,128)(2,1)}) %reduce-scatter.9.cloned.1.call-update) | async-done | bytes 1572880 | tf_op jit(solution)/shard_map/reduce_scatter | solution.py:267
  1640.4 113.6 %reduce-scatter.7.cloned.1.call-done = bf16[1024,768]{0,1:T(8,128)(2,1)} async-done(((bf16[4096,768]{0,1:T(8,128)(2,1)}), bf16[1024,768]{0,1:T(8,128)(2,1)}) %reduce-scatter.7.cloned.1.call-update) | async-done | bytes 1572880 | tf_op jit(solution)/shard_map/reduce_scatter | solution.py:264
  1779.2 21.1 reduce-scatter.13.cloned.1.call-done
  1801.9 78.6 %reduce-scatter.15.cloned.1.call-done = f32[96,3072]{1,0:T(8,128)} async-done(((f32[768,3072]{1,0:T(8,128)}), f32[96,3072]{1,0:T(8,128)}) %reduce-scatter.15.cloned.1.call-update) | async-done | bytes 1179664 | tf_op jit(solution)/shard_map/reduce_scatter | solution.py:241
  1882.6 78.2 %reduce-scatter.17.cloned.1.call-done = f32[384,768]{1,0:T(8,128)} async-done(((f32[3072,768]{1,0:T(8,128)}), f32[384,768]{1,0:T(8,128)}) %reduce-scatter.17.cloned.1.call-update) | async-done | bytes 1179664 | tf_op jit(solution)/shard_map/reduce_scatter | solution.py:242
  1963.0 66.8 %reduce-scatter.11.cloned.1.call-done = f32[96,2304]{1,0:T(8,128)} async-done(((f32[768,2304]{1,0:T(8,128)}), f32[96,2304]{1,0:T(8,128)}) %reduce-scatter.11.cloned.1.call-update) | async-done | bytes 884752 | tf_op jit(solution)/shard_map/reduce_scatter | solution.py:277
  2076.8 32.0 %all-reduce.10.cloned.1.call-done = (bf16[96,2304]{1,0:T(8,128)(2,1)}, bf16[96,768]{1,0:T(8,128)(2,1)}, bf16[96,3072]{1,0:T(8,128)(2,1)}, bf16[384,768]{1,0:T(8,128)(2,1)}) async-done(((bf16[96,2304]{1,0:T(8,128)(2,1)}, bf16[96,768]{1,0:T(8,128)(2,1)}, bf16[96,3072]{1,0:T(8,128)(2,1)}, bf16[384,768]{1,0:T(8,128)(2,1)}), (bf16[96,2304]{1,0:T(8,128)(2,1)}, bf16[96,768]{1,0:T(8,128)(2,1)}, ...) | async-done | bytes 1769488 | tf_op jit(solution)/shard_map/psum | solution.py:282
  (505 shorter events, 1013.2 us)
Async XLA Ops:
  7.2 39.3 %all-gather.7.cloned.1.call-start = ((), (), s32[]{:S(2)}) async-start(), calls=%async_computation.6 | async-start | bytes 3981312 | tf_op jit(solution)/shard_map/all_gather | solution.py:186
  7.9 162.5 %all-gather.11.cloned.1.call-start = ((), (), s32[]{:S(2)}) async-start(), calls=%async_computation.8 | async-start | bytes 7864320 | tf_op jit(solution)/shard_map/all_gather | solution.py:200
  27.3 19.2 copy-start.34
  29.0 23.9 %copy-start.1 = (bf16[1,1024,768]{1,2,0:T(8,128)(2,1)}, bf16[1,1024,768]{1,2,0:T(8,128)(2,1)S(1)}, u32[]{:S(2)}) copy-start(bf16[1,1024,768]{1,2,0:T(8,128)(2,1)S(1)} %copy.30) | copy-start | bytes 4718596
  29.3 17.2 copy-start.26
  30.3 16.2 copy-start.24
  54.9 231.2 %all-gather.9.cloned.1.call-start = ((), (), s32[]{:S(2)}) async-start(), calls=%async_computation.7 | async-start | bytes 7864320 | tf_op jit(solution)/shard_map/all_gather | solution.py:201
  55.6 605.2 %all-gather.13.cloned.1.call-start = ((), (), s32[]{:S(2)}) async-start(), calls=%async_computation.9 | async-start | bytes 1327104 | tf_op jit(solution)/shard_map/all_gather | solution.py:187
  56.2 610.1 %all-gather.15.cloned.1.call-start = ((), (), s32[]{:S(2)}) async-start(), calls=%async_computation.10 | async-start | bytes 5308416 | tf_op jit(solution)/shard_map/all_gather | solution.py:218
  56.8 620.6 %all-gather.17.cloned.1.call-start = ((), (), s32[]{:S(2)}) async-start(), calls=%async_computation.11 | async-start | bytes 5308416 | tf_op jit(solution)/shard_map/all_gather | solution.py:219
  57.3 1583.1 %reduce-scatter.9.cloned.1.call-start = ((), (), s32[]{:S(2)}) async-start(), calls=%async_computation.13 | async-start | bytes 7864320 | tf_op jit(solution)/shard_map/reduce_scatter | solution.py:267
  296.2 364.7 %copy-start.2 = (bf16[1,1024,768]{1,2,0:T(8,128)(2,1)S(1)}, bf16[1,1024,768]{1,2,0:T(8,128)(2,1)}, u32[]{:S(2)}) copy-start(bf16[1,1024,768]{1,2,0:T(8,128)(2,1)} %copy-done.1) | copy-start | bytes 4718596
  664.2 37.9 %copy-start.18 = (f32[1024]{0:T(1024)}, f32[1024]{0:T(1024)S(1)}, u32[]{:S(2)}) copy-start(f32[1024]{0:T(1024)S(1)} %broadcast_multiply_fusion) | copy-start | bytes 12292
  666.2 35.9 %copy-start.22 = (f32[1024]{0:T(1024)}, f32[1024]{0:T(1024)S(1)}, u32[]{:S(2)}) copy-start(f32[1024]{0:T(1024)S(1)} %fusion.70) | copy-start | bytes 12292
  677.4 16.0 copy-start.5
  722.9 24.9 %copy-start.10 = (bf16[4096,128]{0,1:T(8,128)(2,1)}, bf16[4096,128]{0,1:T(8,128)(2,1)S(1)}, u32[]{:S(2)}) copy-start(bf16[4096,128]{0,1:T(8,128)(2,1)S(1)} %constant_dynamic-slice_fusion.21) | copy-start | bytes 3145732 | tf_op jit(solution)/shard_map/while
  857.2 24.9 %copy-start.10 = (bf16[4096,128]{0,1:T(8,128)(2,1)}, bf16[4096,128]{0,1:T(8,128)(2,1)S(1)}, u32[]{:S(2)}) copy-start(bf16[4096,128]{0,1:T(8,128)(2,1)S(1)} %constant_dynamic-slice_fusion.21) | copy-start | bytes 3145732 | tf_op jit(solution)/shard_map/while
  991.6 24.9 %copy-start.10 = (bf16[4096,128]{0,1:T(8,128)(2,1)}, bf16[4096,128]{0,1:T(8,128)(2,1)S(1)}, u32[]{:S(2)}) copy-start(bf16[4096,128]{0,1:T(8,128)(2,1)S(1)} %constant_dynamic-slice_fusion.21) | copy-start | bytes 3145732 | tf_op jit(solution)/shard_map/while
  1125.9 24.9 %copy-start.10 = (bf16[4096,128]{0,1:T(8,128)(2,1)}, bf16[4096,128]{0,1:T(8,128)(2,1)S(1)}, u32[]{:S(2)}) copy-start(bf16[4096,128]{0,1:T(8,128)(2,1)S(1)} %constant_dynamic-slice_fusion.21) | copy-start | bytes 3145732 | tf_op jit(solution)/shard_map/while
  1260.4 24.9 %copy-start.10 = (bf16[4096,128]{0,1:T(8,128)(2,1)}, bf16[4096,128]{0,1:T(8,128)(2,1)S(1)}, u32[]{:S(2)}) copy-start(bf16[4096,128]{0,1:T(8,128)(2,1)S(1)} %constant_dynamic-slice_fusion.21) | copy-start | bytes 3145732 | tf_op jit(solution)/shard_map/while
  1394.6 24.9 %copy-start.10 = (bf16[4096,128]{0,1:T(8,128)(2,1)}, bf16[4096,128]{0,1:T(8,128)(2,1)S(1)}, u32[]{:S(2)}) copy-start(bf16[4096,128]{0,1:T(8,128)(2,1)S(1)} %constant_dynamic-slice_fusion.21) | copy-start | bytes 3145732 | tf_op jit(solution)/shard_map/while
  1531.8 222.3 %reduce-scatter.7.cloned.1.call-start = ((), (), s32[]{:S(2)}) async-start(), calls=%async_computation.12 | async-start | bytes 7864320 | tf_op jit(solution)/shard_map/reduce_scatter | solution.py:264
  1532.6 267.7 %reduce-scatter.13.cloned.1.call-start = ((), (), s32[]{:S(2)}) async-start(), calls=%async_computation.15 | async-start | bytes 2654208 | tf_op jit(solution)/shard_map/reduce_scatter | solution.py:278
  1537.5 343.0 %reduce-scatter.15.cloned.1.call-start = ((), (), s32[]{:S(2)}) async-start(), calls=%async_computation.16 | async-start | bytes 10616832 | tf_op jit(solution)/shard_map/reduce_scatter | solution.py:241
  1548.1 412.7 %reduce-scatter.17.cloned.1.call-start = ((), (), s32[]{:S(2)}) async-start(), calls=%async_computation.17 | async-start | bytes 10616832 | tf_op jit(solution)/shard_map/reduce_scatter | solution.py:242
  1563.1 191.0 %copy-start.3 = (bf16[1,1024,768]{1,2,0:T(8,128)(2,1)S(1)}, bf16[1,1024,768]{1,2,0:T(8,128)(2,1)}, u32[]{:S(2)}) copy-start(bf16[1,1024,768]{1,2,0:T(8,128)(2,1)} %copy-done.1) | copy-start | bytes 4718596
  1563.1 191.0 %copy-start.25 = (f32[1024]{0:T(1024)S(1)}, f32[1024]{0:T(1024)}, u32[]{:S(2)}) copy-start(f32[1024]{0:T(1024)} %copy-done.24) | copy-start | bytes 12292
  1563.1 191.0 %copy-start.27 = (f32[1024]{0:T(1024)S(1)}, f32[1024]{0:T(1024)}, u32[]{:S(2)}) copy-start(f32[1024]{0:T(1024)} %copy-done.26) | copy-start | bytes 12292
  1563.1 191.0 %copy-start.35 = (f32[768]{0:T(1024)S(1)}, f32[768]{0:T(1024)}, u32[]{:S(2)}) copy-start(f32[768]{0:T(1024)} %copy-done.34) | copy-start | bytes 9220
  1563.1 466.6 %reduce-scatter.11.cloned.1.call-start = ((), (), s32[]{:S(2)}) async-start(), calls=%async_computation.14 | async-start | bytes 7962624 | tf_op jit(solution)/shard_map/reduce_scatter | solution.py:277
  1763.4 345.5 %all-reduce.10.cloned.1.call-start = ((), (), s32[]{:S(2)}) async-start(), calls=%async_computation.18 | async-start | bytes 3538944 | tf_op jit(solution)/shard_map/psum | solution.py:282
  2038.6 30.0 %copy-start.31 = (f32[1024]{0:T(1024)S(1)}, f32[1024]{0:T(1024)}, u32[]{:S(2)}) copy-start(f32[1024]{0:T(1024)} %copy-done.30) | copy-start | bytes 12292
  (51 other events, 347.0 us)
Sparse Core Ops, SparseCore 0:
  9.9 36.5 all-gather.6
  55.0 115.3 all-gather.10
  172.5 113.4 all-gather.8
  287.8 22.0 all-gather.12
  311.7 38.7 all-gather.14
  352.2 38.8 all-gather.16
  1531.9 108.4 reduce-scatter.8
  1642.7 111.2 reduce-scatter.6
  1757.4 42.8 reduce-scatter.12
  1803.6 76.8 reduce-scatter.14
  1884.0 76.8 reduce-scatter.16
  1964.2 65.4 reduce-scatter.10
  2033.0 75.8 all-reduce.9
where the time goes:
time: 2130 us; the launch traced here: 2120 us
  matrix products  806 us (38%)
  waiting for transfers between devices  702 us (33%)
  other arithmetic  336 us (16%)
  local copies, waits for them, and re-layouts  179 us (8%)
  loops' own time  42 us (2%)
  blocking collectives  41.5 us (2%)
    dot_general x12, matrix products, one_pair(): jnp.einsum('qhe,khe->hqk', grad_rows, values_pair, preferred_element_type...  224 us
    convert_element_type x12, other arithmetic, one_pair(): (positive * weight_grads - signed * row_dot).astype(jnp.bfloat16)  193 us
    dot_general x12, matrix products, one_pair(): jnp.einsum('hqk,qhe->khe', signed.astype(jnp.bfloat16), grad_rows, prefer...  158 us
    dot_general x12, matrix products, one_pair(): jnp.einsum('hqk,khe->qhe', signed, values_pair, preferred_element_type=jn...  143 us
    dot_general x24, matrix products, one_pair(): jnp.einsum('qhe,khe->hqk', query_rows, keys_pair, preferred_element_type=...  125 us
    reduce_scatter x1, waiting for transfers between devices, per_device(): lax.psum_scatter(key_gradients.astype(jnp.bfloat16), 'ctx', scatter_dimen...  114 us
    all_gather x1, waiting for transfers between devices, per_device(): lax.all_gather(key_local, 'ctx', axis=1, tiled=True)  108 us
    all_gather x1, waiting for transfers between devices, per_device(): lax.all_gather(value_local, 'ctx', axis=1, tiled=True)  107 us
  transfers between devices with their start and end apart: 13, of which 10 were waited for; matrix products, arithmetic and copies ran while one was open for 22% of the time, Pallas kernels for 0%

commit v1 on v0

v1 whole, which is shorter than its diff:
```python
import functools

import jax
import jax.numpy as jnp
from jax import lax
from jax.experimental import pallas as pl
from jax.experimental.pallas import tpu as pltpu
from jax.sharding import PartitionSpec as P

HEAD_DIM = 64
BLK = 512
LOG2E = 1.4426950408889634
BIG = 3e38
LOW = -1e30


def nn(left, right):
    return lax.dot_general(left, right, (((1,), (0,)), ((), ())), preferred_element_type=jnp.float32)


def nt(left, right):
    return lax.dot_general(left, right, (((1,), (1,)), ((), ())), preferred_element_type=jnp.float32)


def sign_of(scores):
    return jnp.tanh(scores.astype(jnp.bfloat16) * jnp.bfloat16(BIG))


def block_mask(key_block, query_block, length):
    keys = key_block * BLK + lax.broadcasted_iota(jnp.int32, (BLK, BLK), 0)
    queries = query_block * BLK + lax.broadcasted_iota(jnp.int32, (BLK, BLK), 1)
    return keys <= jnp.minimum(queries, length - 1)


def split_queries(query_t, weight_ref):
    high = query_t.astype(jnp.bfloat16)
    rest = (query_t - high.astype(jnp.float32)).astype(jnp.bfloat16)
    zero = jnp.zeros((HEAD_DIM, BLK), jnp.bfloat16)
    for head in range(2):
        rows = slice(head * HEAD_DIM, (head + 1) * HEAD_DIM)
        parts = [zero, zero, zero, zero]
        parts[head] = high[rows]
        parts[2 + head] = rest[rows]
        weight_ref[head] = jnp.concatenate(parts, axis=0)


def forward_kernel(table, query_ref, key_ref, value_ref, out_ref, exact_ref, log_ref, value_t, weights):
    length = table[2]
    for part in range(value_ref.shape[0] // BLK):
        rows = slice(part * BLK, (part + 1) * BLK)
        value_t[:, rows] = value_ref[rows, :].T
    for block in range(query_ref.shape[0] // BLK):
        place = table[block]
        rows = slice(block * BLK, (block + 1) * BLK)
        query_t = query_ref[rows, :].astype(jnp.float32).T * (LOG2E * HEAD_DIM ** -0.5)
        split_queries(query_t, weights)
        count = jnp.minimum(place + 1, (length + BLK - 1) // BLK)

        def step(number, carry, masked):
            start = pl.multiple_of(table[4 + number] * BLK, BLK)
            keys = key_ref[pl.ds(start, BLK), :]
            keys = jnp.concatenate([keys, keys], axis=1)
            result = []
            scores_list = [nn(keys, weights[head]) for head in range(2)]
            for head in range(2):
                top, total, mixed = carry[head]
                scores = scores_list[head]
                size = jnp.abs(scores)
                if masked:
                    size = jnp.where(block_mask(number, place, length), size, LOW)
                new_top = jnp.maximum(top, jnp.max(size, axis=0, keepdims=True))
                fade = jnp.exp2(top - new_top)
                powers = jnp.exp2(size - new_top)
                new_total = total * fade + jnp.sum(powers, axis=0, keepdims=True)
                signed = powers.astype(jnp.bfloat16) * sign_of(scores)
                values = value_t[head * HEAD_DIM : (head + 1) * HEAD_DIM, pl.ds(start, BLK)]
                result.append((new_top, new_total, mixed * fade + nn(values, signed)))
            return tuple(result)

        begin = (
            jnp.full((1, BLK), LOW, jnp.float32),
            jnp.zeros((1, BLK), jnp.float32),
            jnp.zeros((HEAD_DIM, BLK), jnp.float32),
        )
        carry = lax.fori_loop(0, count - 1, functools.partial(step, masked=False), (begin, begin))
        carry = step(count - 1, carry, True)
        mixed = jnp.concatenate([c[2] / c[1] for c in carry], axis=0)
        exact_ref[:, rows] = mixed
        out_ref[rows, :] = mixed.T.astype(jnp.bfloat16)
        for head in range(2):
            log_ref[0, head : head + 1, rows] = carry[head][0] + jnp.log2(carry[head][1])


def backward_kernel(
    table,
    query_ref,
    key_ref,
    value_ref,
    grad_ref,
    exact_ref,
    log_ref,
    query_out,
    key_out,
    value_out,
    key_t,
    key_sum,
    value_sum,
    weights,
    grad_weights,
    query_sum,
):
    length = table[2]
    scale = HEAD_DIM ** -0.5
    key_sum[...] = jnp.zeros_like(key_sum)
    value_sum[...] = jnp.zeros_like(value_sum)
    for part in range(key_ref.shape[0] // BLK):
        rows = slice(part * BLK, (part + 1) * BLK)
        key_t[:, rows] = key_ref[rows, :].T
    for block in range(query_ref.shape[0] // BLK):
        place = table[block]
        rows = slice(block * BLK, (block + 1) * BLK)
        query_plain = query_ref[rows, :].astype(jnp.float32).T
        split_queries(query_plain * (LOG2E * scale), weights)
        query_t = query_plain.astype(jnp.bfloat16)
        grad_plain = grad_ref[rows, :].astype(jnp.float32).T
        grad_t = grad_plain.astype(jnp.bfloat16)
        weighted = grad_plain * exact_ref[:, rows]
        zero = jnp.zeros((HEAD_DIM, BLK), jnp.bfloat16)
        grad_weights[0] = jnp.concatenate([grad_t[:HEAD_DIM], zero], axis=0)
        grad_weights[1] = jnp.concatenate([zero, grad_t[HEAD_DIM:]], axis=0)
        dots = [
            jnp.sum(weighted[head * HEAD_DIM : (head + 1) * HEAD_DIM], axis=0, keepdims=True)
            for head in range(2)
        ]
        logs = [log_ref[0, head : head + 1, rows] for head in range(2)]
        query_sum[...] = jnp.zeros_like(query_sum)
        live = place * BLK < length
        count = jnp.where(live, jnp.minimum(place + 1, (length + BLK - 1) // BLK), 0)

        def step(number, masked):
            start = pl.multiple_of(table[4 + number] * BLK, BLK)
            span = pl.ds(start, BLK)
            keys = key_ref[span, :]
            keys = jnp.concatenate([keys, keys], axis=1)
            values = value_ref[span, :]
            scores_list = [nn(keys, weights[head]) for head in range(2)]
            grads_list = [nn(values, grad_weights[head]) for head in range(2)]
            for head in range(2):
                half = slice(head * HEAD_DIM, (head + 1) * HEAD_DIM)
                scores = scores_list[head]
                size = jnp.abs(scores) - logs[head]
                if masked:
                    size = jnp.where(block_mask(number, place, length), size, LOW)
                positive = jnp.exp2(size).astype(jnp.bfloat16)
                sign = sign_of(scores)
                signed = positive * sign
                inner = grads_list[head] - dots[head] * sign.astype(jnp.float32)
                score_grads = (positive.astype(jnp.float32) * inner).astype(jnp.bfloat16)
                value_sum[half, span] += nt(grad_t[half], signed)
                key_sum[half, span] += nt(query_t[half], score_grads)
                query_sum[half, :] += nn(key_t[half, span], score_grads)

        @pl.when(count > 0)
        def _():
            @pl.loop(0, count - 1)
            def _(number):
                step(number, False)

            step(count - 1, True)

        query_out[rows, :] = (query_sum[...] * scale).T.astype(jnp.bfloat16)
    for part in range(key_ref.shape[0] // BLK):
        rows = slice(part * BLK, (part + 1) * BLK)
        key_out[rows, :] = (key_sum[:, rows] * scale).T.astype(jnp.bfloat16)
        value_out[rows, :] = value_sum[:, rows].T.astype(jnp.bfloat16)


def make_table(block_order, length, ctx_index, blocks_here):
    places = lax.dynamic_slice_in_dim(block_order, ctx_index * blocks_here, blocks_here)
    stored = jnp.argsort(block_order).astype(jnp.int32)
    return jnp.concatenate([places, length[None], jnp.zeros((1,), jnp.int32), stored])


def attend_forward(table, packed, pairs_all):
    rows, slots = packed.shape[0], pairs_all.shape[0]
    width = pairs_all.shape[1] // 2
    pairs = width // 128
    return pl.pallas_call(
        forward_kernel,
        grid_spec=pltpu.PrefetchScalarGridSpec(
            num_scalar_prefetch=1,
            grid=(pairs,),
            in_specs=[
                pl.BlockSpec((rows, 128), lambda i, t: (0, i)),
                pl.BlockSpec((slots, 128), lambda i, t: (0, i)),
                pl.BlockSpec((slots, 128), lambda i, t: (0, i + pairs)),
            ],
            out_specs=[
                pl.BlockSpec((rows, 128), lambda i, t: (0, i)),
                pl.BlockSpec((128, rows), lambda i, t: (i, 0)),
                pl.BlockSpec((1, 2, rows), lambda i, t: (i, 0, 0)),
            ],
            scratch_shapes=[
                pltpu.VMEM((128, slots), jnp.bfloat16),
                pltpu.VMEM((2, 256, BLK), jnp.bfloat16),
            ],
        ),
        out_shape=[
            jax.ShapeDtypeStruct((rows, width), jnp.bfloat16),
            jax.ShapeDtypeStruct((width, rows), jnp.float32),
            jax.ShapeDtypeStruct((pairs, 2, rows), jnp.float32),
        ],
        compiler_params=pltpu.CompilerParams(vmem_limit_bytes=48 << 20),
        name="attend_forward",
    )(table, packed, pairs_all, pairs_all)


def attend_backward(table, packed, pairs_all, grad_mixed, exact, logs):
    rows, slots = packed.shape[0], pairs_all.shape[0]
    width = pairs_all.shape[1] // 2
    pairs = width // 128
    return pl.pallas_call(
        backward_kernel,
        grid_spec=pltpu.PrefetchScalarGridSpec(
            num_scalar_prefetch=1,
            grid=(pairs,),
            in_specs=[
                pl.BlockSpec((rows, 128), lambda i, t: (0, i)),
                pl.BlockSpec((slots, 128), lambda i, t: (0, i)),
                pl.BlockSpec((slots, 128), lambda i, t: (0, i + pairs)),
                pl.BlockSpec((rows, 128), lambda i, t: (0, i)),
                pl.BlockSpec((128, rows), lambda i, t: (i, 0)),
                pl.BlockSpec((1, 2, rows), lambda i, t: (i, 0, 0)),
            ],
            out_specs=[
                pl.BlockSpec((rows, 128), lambda i, t: (0, i)),
                pl.BlockSpec((slots, 128), lambda i, t: (0, i)),
                pl.BlockSpec((slots, 128), lambda i, t: (0, i)),
            ],
            scratch_shapes=[
                pltpu.VMEM((128, slots), jnp.bfloat16),
                pltpu.VMEM((128, slots), jnp.float32),
                pltpu.VMEM((128, slots), jnp.float32),
                pltpu.VMEM((2, 256, BLK), jnp.bfloat16),
                pltpu.VMEM((2, 128, BLK), jnp.bfloat16),
                pltpu.VMEM((128, BLK), jnp.float32),
            ],
        ),
        out_shape=[
            jax.ShapeDtypeStruct((rows, width), jnp.bfloat16),
            jax.ShapeDtypeStruct((slots, width), jnp.bfloat16),
            jax.ShapeDtypeStruct((slots, width), jnp.bfloat16),
        ],
        compiler_params=pltpu.CompilerParams(vmem_limit_bytes=48 << 20),
        name="attend_backward",
    )(table, packed, pairs_all, pairs_all, grad_mixed, exact, logs)


def layer_norm(values, gain):
    centre = jnp.mean(values, axis=-1, keepdims=True)
    centred = values - centre
    spread = jnp.mean(centred * centred, axis=-1, keepdims=True)
    return centred * lax.rsqrt(spread + 1e-05) * gain


def gelu_tanh(values):
    return jax.nn.gelu(values, approximate=True)


def project(left_operand, right_operand):
    return jnp.einsum(
        "buj,jn->bun", left_operand, right_operand, preferred_element_type=jnp.float32
    )


def project_back(gradient_list, right_operand):
    return jnp.einsum(
        "mzg,og->mzo", gradient_list, right_operand, preferred_element_type=jnp.float32
    )


def weight_grad(left_operand, gradient_list):
    return jnp.einsum(
        "hcb,hct->bt", left_operand, gradient_list, preferred_element_type=jnp.float32
    )


def per_device(
    tokens_in, out_grad, gain_attn, gain_mlp, w_qkv, w_out, w_up, w_down, lengths, block_order
):
    seq_count, local_rows, width = tokens_in.shape
    ctx_index = lax.axis_index("ctx")
    gain_one, w_qkv_all, w_out_all = (
        lax.all_gather(gain_attn, "fsdp", axis=0, tiled=True),
        lax.all_gather(w_qkv, "fsdp", axis=0, tiled=True),
        lax.all_gather(w_out, "fsdp", axis=0, tiled=True),
    )
    offsets = jnp.arange(BLK, dtype=jnp.int32)
    key_places = (block_order[:, :, None] * BLK + offsets[None, None, :]).reshape(seq_count, -1)
    query_places = lax.dynamic_slice_in_dim(key_places, ctx_index * local_rows, local_rows, 1)
    tokens_f = tokens_in.astype(jnp.float32)
    normed_one, norm_one_back = jax.vjp(layer_norm, tokens_f, gain_one.astype(jnp.float32))
    normed_one = normed_one.astype(jnp.bfloat16)
    packed = project(normed_one, w_qkv_all).astype(jnp.bfloat16)
    pairs_all = lax.all_gather(packed[0, :, width:], "ctx", axis=0, tiled=True)
    table = make_table(block_order[0], lengths[0], ctx_index, local_rows // BLK)
    mixture, exact, logs = attend_forward(table, packed[0], pairs_all)
    mixed = mixture[None]
    middle = tokens_f + project(mixed, w_out_all)
    gain_two, w_up_all, w_down_all = (
        lax.all_gather(gain_mlp, "fsdp", axis=0, tiled=True),
        lax.all_gather(w_up, "fsdp", axis=0, tiled=True),
        lax.all_gather(w_down, "fsdp", axis=0, tiled=True),
    )
    normed_two, norm_two_back = jax.vjp(layer_norm, middle, gain_two.astype(jnp.float32))
    normed_two = normed_two.astype(jnp.bfloat16)
    pre_act = project(normed_two, w_up_all)
    activation, gelu_back = jax.vjp(gelu_tanh, pre_act)
    activation = activation.astype(jnp.bfloat16)
    result = (middle + project(activation, w_down_all)).astype(jnp.bfloat16)
    w_up_back, w_down_back = (
        lax.all_gather(w_up, "fsdp", axis=0, tiled=True),
        lax.all_gather(w_down, "fsdp", axis=0, tiled=True),
    )
    live_mask = (query_places < lengths[:, None]).astype(jnp.float32)
    output_gradient = out_grad.astype(jnp.float32) * live_mask[:, :, None]
    grad_z = output_gradient.astype(jnp.bfloat16)
    grad_w_down = weight_grad(activation, grad_z)
    grad_act = project_back(grad_z, w_down_back)
    grad_pre = gelu_back(grad_act)[0].astype(jnp.bfloat16)
    grad_w_up = weight_grad(normed_two, grad_pre)
    grad_normed_two = project_back(grad_pre, w_up_back)
    grad_middle_norm, grad_gain_two = norm_two_back(grad_normed_two)
    mlp_shards = (
        lax.psum_scatter(grad_w_up, "fsdp", scatter_dimension=0, tiled=True),
        lax.psum_scatter(grad_w_down, "fsdp", scatter_dimension=0, tiled=True),
        lax.psum_scatter(grad_gain_two, "fsdp", scatter_dimension=0, tiled=True),
    )
    grad_middle = output_gradient + grad_middle_norm
    w_qkv_back, w_out_back = (
        lax.all_gather(w_qkv, "fsdp", axis=0, tiled=True),
        lax.all_gather(w_out, "fsdp", axis=0, tiled=True),
    )
    grad_branch = grad_middle.astype(jnp.bfloat16)
    grad_w_out = weight_grad(mixed, grad_branch)
    grad_mixed = project_back(grad_branch, w_out_back).astype(jnp.bfloat16)
    query_grads, key_gradients, value_grads = attend_backward(
        table, packed[0], pairs_all, grad_mixed[0], exact, logs
    )
    key_mine = lax.psum_scatter(key_gradients, "ctx", scatter_dimension=0, tiled=True)
    value_mine = lax.psum_scatter(value_grads, "ctx", scatter_dimension=0, tiled=True)
    packed_items = [jnp.concatenate([query_grads, key_mine, value_mine], axis=-1)]
    grad_packed = jnp.stack(packed_items).astype(jnp.bfloat16)
    grad_w_qkv = weight_grad(normed_one, grad_packed)
    grad_normed_one = project_back(grad_packed, w_qkv_back)
    grad_tokens_norm, grad_gain_one = norm_one_back(grad_normed_one)
    grad_tokens = (grad_middle + grad_tokens_norm).astype(jnp.bfloat16)
    attn_shards = (
        lax.psum_scatter(grad_w_qkv, "fsdp", scatter_dimension=0, tiled=True),
        lax.psum_scatter(grad_w_out, "fsdp", scatter_dimension=0, tiled=True),
        lax.psum_scatter(grad_gain_one, "fsdp", scatter_dimension=0, tiled=True),
    )
    summed = (
        lax.psum(attn_shards[0].astype(jnp.bfloat16), "ctx").astype(jnp.float32),
        lax.psum(attn_shards[1].astype(jnp.bfloat16), "ctx").astype(jnp.float32),
        lax.psum(attn_shards[2].astype(jnp.bfloat16), "ctx").astype(jnp.float32),
        lax.psum(mlp_shards[0].astype(jnp.bfloat16), "ctx").astype(jnp.float32),
        lax.psum(mlp_shards[1].astype(jnp.bfloat16), "ctx").astype(jnp.float32),
        lax.psum(mlp_shards[2].astype(jnp.bfloat16), "ctx").astype(jnp.float32),
    )
    return (result, grad_tokens, summed[2], summed[5], summed[0], summed[1], summed[3], summed[4])


def solution(mesh):
    return jax.shard_map(
        per_device,
        mesh=mesh,
        in_specs=(
            P("fsdp", "ctx", None),
            P("fsdp", "ctx", None),
            P("fsdp"),
            P("fsdp"),
            P("fsdp", None),
            P("fsdp", None),
            P("fsdp", None),
            P("fsdp", None),
            P("fsdp"),
            P("fsdp", None),
        ),
        out_specs=(
            P("fsdp", "ctx", None),
            P("fsdp", "ctx", None),
            P("fsdp"),
            P("fsdp"),
            P("fsdp", None),
            P("fsdp", None),
            P("fsdp", None),
            P("fsdp", None),
        ),
        check_vma=False,
    )
```

time: 2130 us -> 1120 us (0.53)
  matrix products: 806 us -> 105 us
  other arithmetic: 336 us -> 28.3 us
  Pallas kernels: 0 us -> 186 us
  local copies, waits for them, and re-layouts: 179 us -> 29.8 us
  loops' own time: 42 us -> 0 us
    dot_general x84 -> x0, matrix products: 701 us -> none  [the longest x12 224 us: one_pair(): jnp.einsum('qhe,khe->hqk', grad_rows, values_pair, preferred_element_type...]
    convert_element_type x12 -> x0, other arithmetic: 193 us -> none  [one_pair(): (positive * weight_grads - signed * row_dot).astype(jnp.bfloat16)]
    pallas_call x0 -> x2, Pallas kernels: none -> 186 us  [the longest x1 117 us: attend_backward(): pl.pallas_call(backward_kernel, grid_spec=pltpu.PrefetchScalarGridSpec(nu...]
    reduce_sum x12 -> x0, other arithmetic: 62.6 us -> none  [one_pair(): row_total = jnp.sum(exponent, axis=-1, keepdims=True)]
    dynamic_slice x36 -> x1, local copies, waits for them, and re-layouts: 56.8 us -> 0.07 us  [make_table(): lax.dynamic_slice_in_dim(block_order, ctx_index * blocks_here, blocks_here)]
    another operation x2 -> x0, loops' own time: 42 us -> none  [the longest x1 26.2 us: attend_forward(): return lax.fori_loop(0, pair_total, one_pair, start)]
    and x12 -> x0, other arithmetic: 36.7 us -> none  [one_pair(): allowed = (key_places[None, :] <= row_places[:, None]) & key_live[None, :]]
    while x108 -> x0, local copies, waits for them, and re-layouts: 34.7 us -> none
  transfers between devices with their start and end apart: 13 -> 12, of which waited for: 10 -> 10; matrix products, arithmetic and copies ran while one was open for 22% -> 10% of each run, Pallas kernels for 0% -> 6%
where the time goes in v1:
time: 1120 us
  waiting for transfers between devices  712 us (64%)
  Pallas kernels  186 us (17%)
  matrix products  105 us (9%)
  blocking collectives  41.4 us (4%)
  local copies, waits for them, and re-layouts  29.8 us (3%)
  other arithmetic  28.3 us (3%)
  between operations  16.7 us (1%)
    all_gather x1, waiting for transfers between devices, per_device(): pairs_all = lax.all_gather(packed[0, :, width:], 'ctx', axis=0, tiled=True)  213 us
    pallas_call x1, Pallas kernels, attend_backward(): pl.pallas_call(backward_kernel, grid_spec=pltpu.PrefetchScalarGridSpec(nu...  117 us
    reduce_scatter x1, waiting for transfers between devices, per_device(): lax.psum_scatter(value_grads, 'ctx', scatter_dimension=0, tiled=True)  111 us
    reduce_scatter x1, waiting for transfers between devices, per_device(): lax.psum_scatter(grad_w_up, 'fsdp', scatter_dimension=0, tiled=True)  78.7 us
    reduce_scatter x1, waiting for transfers between devices, per_device(): lax.psum_scatter(grad_w_down, 'fsdp', scatter_dimension=0, tiled=True)  78 us
    reduce_scatter x1, waiting for transfers between devices, per_device(): lax.psum_scatter(key_gradients, 'ctx', scatter_dimension=0, tiled=True)  77.6 us
    pallas_call x1, Pallas kernels, attend_forward(): pl.pallas_call(forward_kernel, grid_spec=pltpu.PrefetchScalarGridSpec(num...  68.7 us
    reduce_scatter x1, waiting for transfers between devices, per_device(): lax.psum_scatter(grad_w_qkv, 'fsdp', scatter_dimension=0, tiled=True)  66.9 us
  transfers between devices with their start and end apart: 12, of which 10 were waited for; matrix products, arithmetic and copies ran while one was open for 10% of the time, Pallas kernels for 6%

profile of v1, /device:TPU:0, one launch (start us, length us, event | category | flops | bytes accessed | tf_op | source)
XLA Modules:
  0.0 1119.8 jit_solution(17416544304619165939)
XLA Ops:
  11.6 15.6 %all-reduce.5 = (bf16[768]{0:T(1024)(128)(2,1)S(1)}, bf16[768]{0:T(1024)(128)(2,1)S(1)}) all-reduce(bf16[768]{0:T(1024)(128)(2,1)S(1)} %dynamic-update-slice, bf16[768]{0:T(1024)(128)(2,1)S(1)} %dynamic-update-slice.1), channel_id=1, replica_groups=mesh['ctx'=4,'fsdp'=8] {'fsdp'}, use_global_device_ids=true, to_apply=%add | all-reduce | flops 1536 | bytes 6144
  29.7 16.7 %all-gather.7.cloned.1.call-done = bf16[768,2304]{1,0:T(8,128)(2,1)} async-done(((bf16[96,2304]{1,0:T(8,128)(2,1)}), bf16[768,2304]{1,0:T(8,128)(2,1)}) %all-gather.7.cloned.1.call-update) | async-done | bytes 3538960 | tf_op jit(solution)/shard_map/all_gather | solution.py:295
  46.5 6.3 convolution_convert_fusion.query_ref
  62.7 212.6 %all-gather.15.cloned.1.call-done = bf16[1,4096,1536]{2,1,0:T(8,128)(2,1)} async-done(((bf16[1,1024,1536]{2,1,0:T(8,128)(2,1)}), bf16[1,4096,1536]{2,1,0:T(8,128)(2,1)}) %all-gather.15.cloned.1.call-update) | async-done | bytes 12582928 | tf_op jit(solution)/shard_map/all_gather | solution.py:305
  275.3 68.7 %attend_forward.1 = (bf16[1024,768]{1,0:T(8,128)(2,1)S(1)}, f32[768,1024]{1,0:T(8,128)S(1)}, f32[6,2,1024]{2,1,0:T(2,128)S(1)}) custom-call(s32[12]{0:T(128)S(1)} %pad_add_fusion.table, bf16[1024,2304]{1,0:T(8,128)(2,1)} %copy-done.3, bf16[4096,1536]{1,0:T(8,128)(2,1)} %bitcast.73, bf16[4096,1536]{1,0:T(8,128)(2,1)} %bitcast.74), custom_call_target="tpu_custom_call" | custom-call | tf_op jit(solution)/shard_map/attend_forward/pallas_call | solution.py:188
  345.7 2.8 fusion.42
  350.6 11.1 fusion.38
  361.7 18.8 %all-gather.13.cloned.1.call-done = bf16[3072,768]{1,0:T(8,128)(2,1)} async-done(((bf16[384,768]{1,0:T(8,128)(2,1)}), bf16[3072,768]{1,0:T(8,128)(2,1)}) %all-gather.13.cloned.1.call-update) | async-done | bytes 4718608 | tf_op jit(solution)/shard_map/all_gather | solution.py:313
  380.6 16.2 %fusion.6 = bf16[1024,3072]{1,0:T(8,128)(2,1)} fusion(f32[1024,3072]{1,0:T(8,128)} %fusion.38, bf16[3072,768]{1,0:T(8,128)(2,1)} %all-gather.13.cloned.1.call-done, bf16[1,1024,768]{1,2,0:T(8,128)(2,1)S(1)} %copy-done.7, f32[1024]{0:T(1024)S(1)} %bitcast.78), kind=kOutput, calls=%fused_computation.8 | convolution fusion | flops 4897112064 | bytes 25169920 | tf_op jit(solution)/shard_map/mzg,og->mzo/dot_general | solution.py:277
  396.8 7.8 fusion.17
  409.7 116.8 %attend_backward.1 = (bf16[1024,768]{1,0:T(8,128)(2,1)S(1)}, bf16[4096,768]{1,0:T(8,128)(2,1)}, bf16[4096,768]{1,0:T(8,128)(2,1)}) custom-call(s32[12]{0:T(128)S(1)} %pad_add_fusion.table, bf16[1024,2304]{1,0:T(8,128)(2,1)} %copy-done.3, bf16[4096,1536]{1,0:T(8,128)(2,1)} %bitcast.75, bf16[4096,1536]{1,0:T(8,128)(2,1)} %bitcast.76, ...), custom_call_target="tpu_custom_call" | custom-call | tf_op jit(solution)/shard_map/attend_backward/pallas_call | solution.py:222
  527.3 4.3 fusion.43
  531.7 11.4 %fusion.36 = f32[768,3072]{1,0:T(8,128)} fusion(bf16[1024,3072]{1,0:T(8,128)(2,1)} %fusion.6, f32[1,1024,768]{1,2,0:T(8,128)} %copy-done.4, f32[768]{0:T(1024)S(1)} %convert_element_type.90, f32[1024]{0:T(1024)S(1)} %fusion.34, f32[1024]{0:T(1024)S(1)} %broadcast_multiply_fusion), kind=kOutput, calls=%fused_computation.69 | convolution fusion | flops 4834983936 | bytes 18885632 | tf_op jit(solution)/shard_map/hcb,hct->bt/dot_general | solution.py:283
  544.5 13.9 %fusion.26 = f32[3072,768]{1,0:T(8,128)} fusion(bf16[1,1024,768]{1,2,0:T(8,128)(2,1)S(1)} %copy-done.8, f32[1024]{0:T(1024)S(1)} %bitcast.80, f32[1024,3072]{1,0:T(8,128)} %fusion.38), kind=kOutput, calls=%fused_computation.44 | convolution fusion | flops 4862509056 | bytes 23597056 | tf_op jit(solution)/shard_map/hcb,hct->bt/dot_general | solution.py:283
  559.8 77.6 %reduce-scatter.7.cloned.1.call-done = bf16[1024,768]{1,0:T(8,128)(2,1)} async-done(((bf16[4096,768]{1,0:T(8,128)(2,1)}), bf16[1024,768]{1,0:T(8,128)(2,1)}) %reduce-scatter.7.cloned.1.call-update) | async-done | bytes 1572880 | tf_op jit(solution)/shard_map/reduce_scatter | solution.py:350
  637.4 2.7 constant_dynamic-update-slice_fusion.1
  640.1 110.9 %reduce-scatter.9.cloned.1.call-done = bf16[1024,768]{1,0:T(8,128)(2,1)} async-done(((bf16[4096,768]{1,0:T(8,128)(2,1)}), bf16[1024,768]{1,0:T(8,128)(2,1)}) %reduce-scatter.9.cloned.1.call-update) | async-done | bytes 1572880 | tf_op jit(solution)/shard_map/reduce_scatter | solution.py:351
  751.0 2.8 constant_dynamic-update-slice_fusion
  753.8 8.4 fusion.30
  763.0 12.5 %fusion.19 = bf16[1,1024,768]{1,2,0:T(8,128)(2,1)} fusion(f32[1,1024,768]{1,2,0:T(8,128)} %copy-done.4, bf16[3072,768]{1,0:T(8,128)(2,1)} %all-gather.13.cloned.1.call-done, f32[1024,3072]{1,0:T(8,128)} %fusion.38), kind=kOutput, calls=%fused_computation.31 | convolution fusion | flops 4861722624 | bytes 22020096 | tf_op jit(solution)/shard_map/buj,jn->bun/dot_general | solution.py:271
  775.5 2.8 copy.26
  778.2 19.0 %reduce-scatter.13.cloned.1.call-done = f32[96,768]{1,0:T(8,128)} async-done(((f32[768,768]{1,0:T(8,128)}), f32[96,768]{1,0:T(8,128)}) %reduce-scatter.13.cloned.1.call-update) | async-done | bytes 294928 | tf_op jit(solution)/shard_map/reduce_scatter | solution.py:360
  798.9 78.7 %reduce-scatter.15.cloned.1.call-done = f32[96,3072]{1,0:T(8,128)} async-done(((f32[768,3072]{1,0:T(8,128)}), f32[96,3072]{1,0:T(8,128)}) %reduce-scatter.15.cloned.1.call-update) | async-done | bytes 1179664 | tf_op jit(solution)/shard_map/reduce_scatter | solution.py:335
  879.8 78.0 %reduce-scatter.17.cloned.1.call-done = f32[384,768]{1,0:T(8,128)} async-done(((f32[3072,768]{1,0:T(8,128)}), f32[384,768]{1,0:T(8,128)}) %reduce-scatter.17.cloned.1.call-update) | async-done | bytes 1179664 | tf_op jit(solution)/shard_map/reduce_scatter | solution.py:336
  960.0 66.9 %reduce-scatter.11.cloned.1.call-done = f32[96,2304]{1,0:T(8,128)} async-done(((f32[768,2304]{1,0:T(8,128)}), f32[96,2304]{1,0:T(8,128)}) %reduce-scatter.11.cloned.1.call-update) | async-done | bytes 884752 | tf_op jit(solution)/shard_map/reduce_scatter | solution.py:359
  1028.9 9.0 fusion.16
  1037.9 3.2 fusion.14
  1041.0 13.6 %all-reduce.4 = (bf16[768]{0:T(1024)(128)(2,1)S(1)}, bf16[768]{0:T(1024)(128)(2,1)S(1)}) all-reduce(f32[768]{0:T(1024)S(1)} %get-tuple-element.40, f32[768]{0:T(1024)S(1)} %get-tuple-element.38), channel_id=5, replica_groups=mesh['ctx'=4,'fsdp'=8] {'fsdp'}, use_global_device_ids=true, to_apply=%region_12.13.clone | all-reduce | flops 1536 | bytes 9216
  1054.7 12.3 %all-reduce.6 = (bf16[96]{0:T(256)(128)(2,1)S(1)}, bf16[96]{0:T(256)(128)(2,1)S(1)}) all-reduce(bf16[96]{0:T(256)(128)(2,1)S(1)} %dynamic-slice.10, bf16[96]{0:T(256)(128)(2,1)S(1)} %dynamic-slice.9), channel_id=1, replica_groups=mesh['ctx'=4,'fsdp'=8] {'ctx'}, use_global_device_ids=true, to_apply=%region_13.14 | all-reduce | flops 192 | bytes 768 | tf_op jit(solution)/shard_map/psum | solution.py:366
  1068.0 5.6 add_convert_fusion
  1073.6 2.6 copy.27
  1076.2 29.6 %all-reduce.10.cloned.1.call-done = (bf16[96,2304]{1,0:T(8,128)(2,1)}, bf16[96,768]{1,0:T(8,128)(2,1)}, bf16[96,3072]{1,0:T(8,128)(2,1)}, bf16[384,768]{1,0:T(8,128)(2,1)}) async-done(((bf16[96,2304]{1,0:T(8,128)(2,1)}, bf16[96,768]{1,0:T(8,128)(2,1)}, bf16[96,3072]{1,0:T(8,128)(2,1)}, bf16[384,768]{1,0:T(8,128)(2,1)}), (bf16[96,2304]{1,0:T(8,128)(2,1)}, bf16[96,768]{1,0:T(8,128)(2,1)}, ...) | async-done | bytes 1769488 | tf_op jit(solution)/shard_map/psum | solution.py:364
  (106 shorter events, 43.9 us)
Async XLA Ops:
  7.2 39.3 %all-gather.7.cloned.1.call-start = ((), (), s32[]{:S(2)}) async-start(), calls=%async_computation.6 | async-start | bytes 3981312 | tf_op jit(solution)/shard_map/all_gather | solution.py:295
  7.9 267.4 %all-gather.15.cloned.1.call-start = ((), (), s32[]{:S(2)}) async-start(), calls=%async_computation.16 | async-start | bytes 15728640 | tf_op jit(solution)/shard_map/all_gather | solution.py:305
  29.0 316.7 %copy-start.1 = (bf16[1,1024,768]{1,2,0:T(8,128)(2,1)}, bf16[1,1024,768]{1,2,0:T(8,128)(2,1)S(1)}, u32[]{:S(2)}) copy-start(bf16[1,1024,768]{1,2,0:T(8,128)(2,1)S(1)} %copy.23) | copy-start | bytes 4718596
  29.7 23.1 %copy-start.13 = (f32[1024]{0:T(1024)}, f32[1024]{0:T(1024)S(1)}, u32[]{:S(2)}) copy-start(f32[1024]{0:T(1024)S(1)} %fusion.15) | copy-start | bytes 12292
  52.8 2.1 copy-start.3
  56.9 2.9 copy-start.10
  56.9 4.5 copy-start.16
  57.0 288.7 %all-gather.9.cloned.1.call-start = ((), (), s32[]{:S(2)}) async-start(), calls=%async_computation.7 | async-start | bytes 1327104 | tf_op jit(solution)/shard_map/all_gather | solution.py:296
  57.7 292.8 %all-gather.11.cloned.1.call-start = ((), (), s32[]{:S(2)}) async-start(), calls=%async_computation.8 | async-start | bytes 5308416 | tf_op jit(solution)/shard_map/all_gather | solution.py:312
  58.3 322.3 %all-gather.13.cloned.1.call-start = ((), (), s32[]{:S(2)}) async-start(), calls=%async_computation.9 | async-start | bytes 5308416 | tf_op jit(solution)/shard_map/all_gather | solution.py:313
  58.9 578.5 %reduce-scatter.7.cloned.1.call-start = ((), (), s32[]{:S(2)}) async-start(), calls=%async_computation.10 | async-start | bytes 7864320 | tf_op jit(solution)/shard_map/reduce_scatter | solution.py:350
  344.1 1.6 copy-start
  348.5 1.6 copy-start.4
  350.5 30.0 %copy-start.7 = (bf16[1,1024,768]{1,2,0:T(8,128)(2,1)S(1)}, bf16[1,1024,768]{1,2,0:T(8,128)(2,1)}, u32[]{:S(2)}) copy-start(bf16[1,1024,768]{1,2,0:T(8,128)(2,1)} %copy.25) | copy-start | bytes 4718596
  380.6 16.2 %copy-start.5 = (f32[1,1024,768]{1,2,0:T(8,128)S(1)}, f32[1,1024,768]{1,2,0:T(8,128)}, u32[]{:S(2)}) copy-start(f32[1,1024,768]{1,2,0:T(8,128)} %copy-done.4) | copy-start | bytes 9437188
  380.6 16.2 %copy-start.9 = (bf16[768,3072]{1,0:T(8,128)(2,1)S(1)}, bf16[768,3072]{1,0:T(8,128)(2,1)}, u32[]{:S(2)}) copy-start(bf16[768,3072]{1,0:T(8,128)(2,1)} %all-gather.11.cloned.1.call-done) | copy-start | bytes 14155780
  405.3 1.6 copy-start.6
  407.0 1.3 copy-start.15
  408.3 1.5 copy-start.11
  526.5 224.5 %reduce-scatter.9.cloned.1.call-start = ((), (), s32[]{:S(2)}) async-start(), calls=%async_computation.11 | async-start | bytes 7864320 | tf_op jit(solution)/shard_map/reduce_scatter | solution.py:351
  527.3 270.0 %reduce-scatter.13.cloned.1.call-start = ((), (), s32[]{:S(2)}) async-start(), calls=%async_computation.13 | async-start | bytes 2654208 | tf_op jit(solution)/shard_map/reduce_scatter | solution.py:360
  531.6 346.0 %reduce-scatter.15.cloned.1.call-start = ((), (), s32[]{:S(2)}) async-start(), calls=%async_computation.14 | async-start | bytes 10616832 | tf_op jit(solution)/shard_map/reduce_scatter | solution.py:335
  543.1 1.4 copy-start.8
  543.1 414.7 %reduce-scatter.17.cloned.1.call-start = ((), (), s32[]{:S(2)}) async-start(), calls=%async_computation.15 | async-start | bytes 10616832 | tf_op jit(solution)/shard_map/reduce_scatter | solution.py:336
  558.5 468.4 %reduce-scatter.11.cloned.1.call-start = ((), (), s32[]{:S(2)}) async-start(), calls=%async_computation.12 | async-start | bytes 7962624 | tf_op jit(solution)/shard_map/reduce_scatter | solution.py:359
  559.8 194.0 %copy-start.2 = (bf16[1,1024,768]{1,2,0:T(8,128)(2,1)S(1)}, bf16[1,1024,768]{1,2,0:T(8,128)(2,1)}, u32[]{:S(2)}) copy-start(bf16[1,1024,768]{1,2,0:T(8,128)(2,1)} %copy-done.1) | copy-start | bytes 4718596
  762.3 343.6 %all-reduce.10.cloned.1.call-start = ((), (), s32[]{:S(2)}) async-start(), calls=%async_computation.17 | async-start | bytes 3538944 | tf_op jit(solution)/shard_map/psum | solution.py:364
  1028.9 9.0 copy-start.14
  1105.8 5.9 copy-start.12
Sparse Core Ops, SparseCore 0:
  9.9 36.5 all-gather.6
  57.1 218.1 all-gather.14
  277.2 22.2 all-gather.8
  301.2 38.7 all-gather.10
  341.7 38.7 all-gather.12
  526.6 110.7 reduce-scatter.6
  639.7 111.2 reduce-scatter.8
  754.4 42.8 reduce-scatter.12
  800.8 76.8 reduce-scatter.14
  881.0 76.8 reduce-scatter.16
  961.3 65.4 reduce-scatter.10
  1029.9 75.8 all-reduce.9
